TPU v7x, 32 devices: a whole 2x2x4 slice. The times are simulated.
32 devices in a mesh: lon: 8 (over z, x), lat: 4 (over y, core).
Axes of the slice: x: 2, y: 2, z: 4, core: 2. Of those that a mesh axis runs over, the one named last changes fastest.
Arguments:
- tracers: float32 [40, 8, 32, 1024], P(None, None, 'lat', 'lon'), may hold values from -6 to 6
- kmt: int32 [32, 1024], P('lat', 'lon'), may hold values from 0 to 8
Outputs:
- updated: float32 [40, 8, 32, 1024], P(None, None, 'lat', 'lon')
Inputs may be any that keep to these rules, and one draw needn't show every extreme that they name: Level k of column (j, i) is ocean exactly when k < kmt[j, i].
All inputs are finite; a program needn't handle non-finite values.
Results may differ from a plain program's by a relative error of at most 0.00002.
Values sent between devices are 32-bit elements; how exact they have to be, the bound alone decides.
A program may use at most 64 MiB of HBM per device.

v0:
```python
import functools

import jax
import jax.numpy as jnp
from jax import lax
from jax.experimental import pallas as pl
from jax.experimental.pallas import tpu as pltpu
from jax.sharding import PartitionSpec as P

THERMAL = 0.2
HALINE = 0.8
REDI = 0.1
SKEW = 0.05
SLOPE_MAX = 0.6
SLOPE_WIDTH = 0.2

MESH = pl.DeviceIdType.MESH
TOGETHER = 2
STORE = 2
EARLY = 2
C, E, W, N, S = range(5)


def taper(slope):
    return slope * 0.5 * (1.0 + jnp.tanh((SLOPE_MAX - jnp.abs(slope)) / SLOPE_WIDTH))


def column(rho, wet, up, dn):
    hi = wet * dn(wet)
    strat = (dn(rho) - rho) * hi
    return rho, wet, hi, up(hi), 0.5 * (strat + up(strat))


def line(c, p, m, up, dn):
    c_rho, c_wet, c_hi, c_lo, c_cell = c
    p_rho, p_wet, p_hi, p_lo, p_cell = p
    m_rho, m_wet, m_hi, m_lo, m_cell = m
    mp, mm = c_wet * p_wet, c_wet * m_wet
    sp = taper((p_rho - c_rho) * mp / jnp.maximum(0.5 * (p_cell + c_cell), 1.0))
    sm = taper((c_rho - m_rho) * mm / jnp.maximum(0.5 * (m_cell + c_cell), 1.0))
    cx = 0.5 * (sp + sm)
    sw = 0.5 * (cx + dn(cx))
    fh = ((REDI + SKEW) * 0.25) * sw * c_hi
    zh = REDI * (sw * sw) * c_hi
    fl, zl = up(fh), up(zh)
    pp = ((REDI - SKEW) * 0.25) * sp * mp
    pm = -((REDI - SKEW) * 0.25) * sm * mm
    own_p, own_m = mp * (fh - fl), mm * (fl - fh)
    mph, mmh = dn(mp) * fh, dn(mm) * fh
    mpl, mml = up(mp) * fl, up(mm) * fl
    q = pp + pm
    return (
        (mpl - mml - q * c_lo + zl,
         q * (c_lo - c_hi) - REDI * (mp + mm) - (own_p + own_m) - (zh + zl),
         mmh - mph + q * c_hi + zh),
        (-pp * p_lo - mpl, REDI * mp + pp * (p_lo - p_hi) + own_p, pp * p_hi + mph),
        (mml - pm * m_lo, REDI * mm + pm * (m_lo - m_hi) + own_m, pm * m_hi - mmh),
    )


def total(terms):
    result = terms[0]
    for term in terms[1:]:
        result = result + term
    return result


def pick(value, index):
    return jnp.take_along_axis(value, index, axis=1)


def up3(v):
    return jnp.concatenate([jnp.zeros_like(v[:1]), v[:-1]], axis=0)


def dn3(v):
    return jnp.concatenate([v[1:], jnp.zeros_like(v[:1])], axis=0)


def applied(c, v):
    return c[1] * v + c[0] * up3(v) + c[2] * dn3(v)


def layout(tracers, split, levels, lanes):
    slots = (split + 2, tracers - split)
    pers = tuple((lanes - 2) // slot for slot in slots)
    return slots, pers, tuple((levels + per - 1) // per for per in pers)


def tracer_of(lane, lanes, tracers):
    return jnp.minimum((lane + 1) // 2 % (lanes // 2), tracers - 1)


def both(refs, offs, at, reg):
    rows, lanes = at.shape
    span = pl.ds(reg * rows, rows)
    west_side = lax.broadcasted_iota(jnp.int32, at.shape, 1) % 2 == 0
    picked = [pick(ref[span, :], (at + off + lanes) % lanes) for ref, off in zip(refs, offs)]
    return jnp.where(west_side, *picked)


def values_of(refs, offs, spot, per, slot, first, levels):
    return jnp.stack([both(refs, offs, k % per * slot + spot, first + k // per) for k in range(levels)])


def kernel(sizes, x_ref, kmt_ref, out_ref, add_ref, tab_ref, halo2, *scratch):
    pl.run_scoped(
        functools.partial(body, sizes, x_ref, kmt_ref, out_ref, add_ref, tab_ref, halo2, *scratch),
        pltpu.SemaphoreType.DMA((len(sizes[-1]) + 1,)),
        pltpu.SemaphoreType.DMA((5,)),
    )


def body(
    sizes, x_ref, kmt_ref, out_ref, add_ref, tab_ref, halo2,
    xv, kmt_int, coef, wcol, ecol, inner_w, inner_e, relay, halo1, from_n, from_s,
    recv_sem, load_sem, send_sem,
):
    tracers, levels, rows, lanes, n_lon, n_lat, groups = sizes
    lon, lat = lax.axis_index("lon"), lax.axis_index("lat")
    at_top = lat == n_lat - 1
    below_top = jnp.logical_not(at_top)
    inner = lat > 0
    at_bottom = jnp.logical_not(inner)
    even_lat = jnp.logical_and(inner, jnp.logical_and(lat % 2 == 0, below_top))
    odd_lat = jnp.logical_and(lat > 1, lat % 2 == 1)
    relayed = jnp.logical_and(lon == 0, even_lat)
    relays = jnp.logical_and(lon == 0, odd_lat)
    far = jnp.logical_and(lon == n_lon - 1, even_lat)
    direct, near = jnp.logical_not(relayed), jnp.logical_not(far)
    early = jnp.logical_and(lon == 0, direct)
    late = jnp.logical_not(early)
    late_top, late_below = jnp.logical_and(late, at_top), jnp.logical_and(late, below_top)
    e_dev = (lax.rem(lon + 1, n_lon), lat)
    w_dev = (lax.rem(lon + n_lon - 1, n_lon), lat)
    n_dev, s_dev = (lon, lat + 1), (lon, lat - 1)
    lat_up, lat_down = lax.rem(lat + 1, n_lat), lax.rem(lat + n_lat - 1, n_lat)
    fold_dev = (n_lon - 1 - lon, lat)
    tiles = tracers * levels
    plane = levels * rows
    lead = levels
    ends = [sum(groups[:i]) for i in range(len(groups) + 1)]
    split = ends[-2]
    slots, pers, shares = layout(tracers, split, levels, lanes)
    kmt_at = pers[0] * slots[0]

    load_kmt = pltpu.make_async_copy(kmt_ref, kmt_int, load_sem.at[len(groups)])
    load_kmt.start()

    def load(first, count, i):
        return pltpu.make_async_copy(
            x_ref.at[pl.ds(first, count)], xv.at[pl.ds(lead + first, count)], load_sem.at[i]
        )

    for i in range(len(groups)):
        for t in range(ends[i], ends[i + 1]):
            load(t * levels, levels, i).start()
    loads = [load(ends[i] * levels, groups[i] * levels, i) for i in range(len(groups))]
    flat = xv.reshape((lead + tiles) * rows, lanes)

    barrier = pltpu.get_barrier_semaphore()

    def greet(dev):
        pl.semaphore_signal(barrier, inc=1, device_id=dev, device_id_type=MESH)

    with jax.named_scope("greet"):
        greet(w_dev)

        @pl.when(near)
        def _():
            greet(e_dev)

        @pl.when(far)
        def _():
            greet((0, lat_up))

        @pl.when(at_top)
        def _():
            greet(fold_dev)

        @pl.when(below_top)
        def _():
            greet(n_dev)

        @pl.when(inner)
        def _():
            greet(s_dev)

    lane = lax.broadcasted_iota(jnp.int32, (rows, lanes), 1)
    row = lax.broadcasted_iota(jnp.int32, (rows, lanes), 0)

    def send(src, dst, s, r, dev):
        return pltpu.make_async_remote_copy(
            src_ref=src, dst_ref=dst, send_sem=send_sem.at[s], recv_sem=recv_sem.at[r],
            device_id=dev, device_id_type=MESH,
        )

    def rows_of(r, span, dst, s, into, dev):
        return send(xv.at[span, r, :], dst.at[span], s, into, dev)

    cut = lead + ends[-2] * levels
    starts = [lead - 1] + [lead + e * levels for e in ends[1:]]
    spans = [pl.ds(a, b - a) for a, b in zip(starts, starts[1:])]
    every = pl.ds(lead - 1, tiles + 1)
    halves = [(pl.ds(lead - 1, cut - lead + 1), 0), (spans[-1], 5)]
    fold = rows_of(rows - 1, every, from_n, 0, 0, fold_dev)
    folds = [
        rows_of(rows - 1, span, from_n, 0, 5 if i == len(spans) - 1 else 0, fold_dev)
        for i, span in enumerate(spans)
    ]
    to_n = rows_of(rows - 1, every, from_s, 0, 1, n_dev)
    to_s = rows_of(0, every, from_n, 1, 0, s_dev)
    to_ss = [rows_of(0, span, from_n, 1, r, s_dev) for span, r in halves]
    cols = (pl.ds(0, shares[0] * rows), pl.ds(shares[0] * rows, shares[1] * rows))
    halos = (halo1, halo2)
    wests = [h.at[pl.ds(0, n * rows)] for h, n in zip(halos, shares)]
    easts = [h.at[pl.ds(n * rows, n * rows)] for h, n in zip(halos, shares)]
    far_dev = (n_lon - 1, lat_down)
    to_e = [send(ecol.at[c], wests[i], 2, 2 + i, e_dev) for i, c in enumerate(cols)]
    to_w = [send(wcol.at[c], easts[i], 3, 2 + i, w_dev) for i, c in enumerate(cols)]
    onward = [send(relay.at[c], easts[i], 4, 2 + i, far_dev) for i, c in enumerate(cols)]
    to_relay = send(wcol, relay, 3, 4, (lon, lat_up))
    got = [send(h, h, 2, 2 + i, e_dev) for i, h in enumerate(halos)]
    all_e, all_w, all_onward = (send(c, relay, s, 4, e_dev) for c, s in ((ecol, 2), (wcol, 3), (relay, 4)))

    def tile(t, k):
        return flat[pl.ds(lead * rows + t * plane + k * rows, rows), :]

    def density(k):
        return HALINE * tile(1, k) - THERMAL * tile(0, k)

    def where_is(t, k):
        n, u = (0, t) if t < split else (1, t - split)
        return k % pers[n] * slots[n] + u, n * shares[0] + k // pers[n]

    def gather_columns(e_ref, w_ref, e_off, w_off, before=None, after=None):
        zeros = jnp.zeros((rows, lanes), jnp.float32)
        es, ws = [zeros] * sum(shares), [zeros] * sum(shares)

        def place(value, at, reg):
            value = pltpu.roll(value, at + 1, 1)
            es[reg] = jnp.where(lane == (at + e_off) % lanes, value, es[reg])
            ws[reg] = jnp.where(lane == (at + w_off) % lanes, value, ws[reg])

        for i in range(len(groups)):
            if before is not None:
                before(i)
            if i == 0:
                place(kmt_own, kmt_at, 0)
                for k in range(levels):
                    at, reg = where_is(0, k)
                    place(density(k), at + split, reg)
            for t in range(ends[i], ends[i + 1]):
                for k in range(levels):
                    place(tile(t, k), *where_is(t, k))
            if ends[i + 1] in (split, tracers):
                n = 0 if ends[i + 1] == split else 1
                for j in range(n * shares[0], n * shares[0] + shares[n]):
                    e_ref[pl.ds(j * rows, rows), :] = es[j]
                    w_ref[pl.ds(j * rows, rows), :] = ws[j]
                if after is not None:
                    after(n)

    def enter():
        @pl.when(at_bottom)
        def _():
            pl.semaphore_wait(barrier, 3)

        @pl.when(jnp.logical_and(inner, jnp.logical_not(jnp.logical_or(relayed, relays))))
        def _():
            pl.semaphore_wait(barrier, 4)

        @pl.when(relayed)
        def _():
            pl.semaphore_wait(barrier, 3)

        @pl.when(relays)
        def _():
            pl.semaphore_wait(barrier, 5)

    def send_inner_rows():
        @pl.when(below_top)
        def _():
            to_n.start()

        @pl.when(inner)
        def _():
            for copy in to_ss:
                copy.start()

    def before(i):
        with jax.named_scope(f"load{i}"):
            loads[i].wait()
        if i == 0:

            @pl.when(late_top)
            def _():
                enter()

        if i < len(groups) - 1:

            @pl.when(late_top)
            def _():
                folds[i].start()

    def after(n):
        if n == 0:

            @pl.when(late_below)
            def _():
                with jax.named_scope("barrier"):
                    enter()

        @pl.when(late)
        def _():
            to_e[n].start()

        @pl.when(jnp.logical_and(late, direct))
        def _():
            to_w[n].start()

    with jax.named_scope("loadk"):
        load_kmt.wait()
    kmt_own = kmt_int[...].astype(jnp.float32)
    xv[lead - 1, :, :] = kmt_own
    gather_columns(ecol, wcol, 0, 1, before, after)
    with jax.named_scope("send"):

        @pl.when(relayed)
        def _():
            to_relay.start()

        @pl.when(late_top)
        def _():
            folds[-1].start()

        @pl.when(late)
        def _():
            send_inner_rows()

    with jax.named_scope("inner"):
        gather_columns(inner_e, inner_w, -1, 2)

        @pl.when(at_bottom)
        def _():
            for t in range(tracers + 1):
                from_s[pl.ds(t * levels, levels), :] = jnp.zeros((levels, lanes), jnp.float32)

    def put(d, dk, k, value):
        coef[pl.ds(((d * 3 + dk) * levels + k) * rows, rows), :] = value

    def piece_of(d, dk, k):
        return coef[pl.ds(((d * 3 + dk) * levels + k) * rows, rows), :]

    with jax.named_scope("coefs"):
        def shifted(v, by, axis):
            return jnp.stack([pltpu.roll(v[k], by, axis) for k in range(levels)])

        own_rho = jnp.stack([density(k) for k in range(levels)])
        own_wet = jnp.stack([(kmt_own > float(k)).astype(jnp.float32) for k in range(levels)])
        c3 = column(own_rho, own_wet, up3, dn3)

        def moved(by, axis):
            return tuple(shifted(v, by, axis) for v in c3)

        mid_lane = jnp.logical_and(lane > 0, lane < lanes - 1)
        xc, xe, xw = line(c3, moved(lanes - 1, 1), moved(1, 1), up3, dn3)
        for dk in range(3):
            for k in range(levels):
                put(E, dk, k, jnp.where(mid_lane, xe[dk][k], 0.0))
                put(W, dk, k, jnp.where(mid_lane, xw[dk][k], 0.0))
                put(C, dk, k, jnp.where(mid_lane, xc[dk][k], 0.0))
        mid_row = jnp.logical_and(row > 0, row < rows - 1)
        yc, yn, ys = line(c3, moved(rows - 1, 0), moved(1, 0), up3, dn3)
        for dk in range(3):
            for k in range(levels):
                put(N, dk, k, jnp.where(mid_row, yn[dk][k], 0.0))
                put(S, dk, k, jnp.where(mid_row, ys[dk][k], 0.0))
                core = piece_of(C, dk, k) + jnp.where(mid_row, yc[dk][k], 0.0)
                put(C, dk, k, core + 1.0 if dk == 1 else core)

    with jax.named_scope("main"):

        @pl.loop(0, tracers // TOGETHER)
        def _(i):
            fields = []
            for u in range(TOGETHER):
                base = pl.multiple_of(lead * rows + (i * TOGETHER + u) * plane, rows)
                field = []
                for k in range(levels):
                    own = flat[pl.ds(base + k * rows, rows), :]
                    field.append((
                        own, pltpu.roll(own, lanes - 1, 1), pltpu.roll(own, 1, 1),
                        pltpu.roll(own, rows - 1, 0), pltpu.roll(own, 1, 0),
                    ))
                fields.append(field)
            for k in range(levels):
                sums = [None] * TOGETHER
                for d in range(5):
                    for dk in range(3):
                        if not 0 <= k + dk - 1 < levels:
                            continue
                        c = piece_of(d, dk, k)
                        for u in range(TOGETHER):
                            term = c * fields[u][k + dk - 1][d]
                            sums[u] = term if sums[u] is None else sums[u] + term
                for u in range(TOGETHER):
                    base = pl.multiple_of((i * TOGETHER + u) * plane, rows)
                    out_ref[pl.ds(base + k * rows, rows), :] = sums[u]

    @pl.when(early)
    def _():
        with jax.named_scope("barrier"):
            enter()
        for copy in to_e + to_w:
            copy.start()
        send_inner_rows()

        @pl.when(at_top)
        def _():
            for copy in folds:
                copy.start()

    @pl.when(relays)
    def _():
        to_relay.wait_recv()
        for copy in onward:
            copy.start()

    level = lax.broadcasted_iota(jnp.int32, (levels, lanes), 0)
    level_f = level.astype(jnp.float32)

    def up_s(v):
        return jnp.where(level == 0, 0.0, pltpu.roll(v, 1, 0))

    def dn_s(v):
        return jnp.where(level == levels - 1, 0.0, pltpu.roll(v, levels - 1, 0))

    def at_row(t, r):
        return flat[pl.ds(lead * rows + t * plane + r, levels, stride=rows), :]

    def row_column(t0, t1, kmt):
        wet = (jnp.broadcast_to(kmt, (levels, lanes)) > level_f).astype(jnp.float32)
        return column(HALINE * t1 - THERMAL * t0, wet, up_s, dn_s)

    def own_row(r):
        return row_column(at_row(0, r), at_row(1, r), kmt_own[r : r + 1, :])

    def fix_rows(source, r, r_in, north, turn, parts):
        def halo(t):
            h = source[pl.ds(lead + t * levels, levels), :]
            return pick(h, lanes - 1 - lane) if turn else h

        first, last, wait = parts[0]
        wait()
        k = jnp.broadcast_to(source[pl.ds(lead - 1, 1), :], (rows, lanes))
        k = (pick(k, lanes - 1 - lane) if turn else k)[:1, :]
        out_c, in_c = row_column(halo(0), halo(1), k), own_row(r_in)
        p, m = (out_c, in_c) if north else (in_c, out_c)
        cc, cp, cm = line(own_row(r), p, m, up_s, dn_s)
        c_out, c_in = (cp, cm) if north else (cm, cp)
        table = (cc, c_out, c_in)
        lo = [pltpu.roll(c[0], levels - 1, 0) for c in table]
        mid = [c[1] for c in table]
        hi = [pltpu.roll(c[2], 1, 0) for c in table]
        for n, (first, last, wait) in enumerate(parts):
            if n:
                wait()
            count = last - first
            batch = count if turn else next(b for b in (8, 5, 4, 3, 2, 1) if count % b == 0)

            @pl.loop(0, count // batch)
            def _(i, first=first, batch=batch):
                for u in range(batch):
                    t = first + i * batch + u
                    values = (at_row(t, r), halo(t), at_row(t, r_in))
                    above = total([c * v for c, v in zip(lo, values)])
                    same = total([c * v for c, v in zip(mid, values)])
                    below = total([c * v for c, v in zip(hi, values)])
                    place = pl.ds(t * plane + r, levels, stride=rows)
                    out_ref[place, :] = (
                        out_ref[place, :] + same + pltpu.roll(above, 1, 0) + pltpu.roll(below, levels - 1, 0)
                    )

    def fix_n(turn):
        parts = [(0, ends[-2], to_ss[0].wait_recv), (ends[-2], tracers, to_ss[1].wait_recv)]
        fix_rows(from_n, rows - 1, rows - 2, True, turn, parts)

    with jax.named_scope("fixs"):

        @pl.when(inner)
        def _():
            to_n.wait_recv()

        fix_rows(from_s, 0, 1, False, False, [(0, tracers, lambda: None)])

    with jax.named_scope("fixn"):

        @pl.when(below_top)
        def _():
            fix_n(False)

    spot = tracer_of(lane, lanes, tracers)
    low = spot < split
    spots = (jnp.minimum(spot, split - 1), jnp.maximum(spot - split, 0))

    def part_of(refs, offs, n):
        return values_of(refs, offs, spots[n], pers[n], slots[n], n * shares[0], levels)

    def column_of(refs, offs):
        fixed = jnp.zeros((rows, lanes), jnp.int32)
        rho = jnp.stack([both(refs, offs, fixed + (where_is(0, k)[0] + split), where_is(0, k)[1])
                         for k in range(levels)])
        kmt = both(refs, offs, fixed + kmt_at, 0)
        wet = jnp.stack([(kmt > float(k)).astype(jnp.float32) for k in range(levels)])
        return column(rho, wet, up3, dn3)

    def joined(first, second):
        return jnp.stack([jnp.where(low, first[k], second[k]) for k in range(levels)])

    with jax.named_scope("fixc0"):
        own_at, ins_at, outs_at = ((wcol, ecol), (1, 0)), ((inner_w, inner_e), (2, -1)), ((wests[0], easts[0]), (0, 1))
        own_c, ins_c = column_of(*own_at), column_of(*ins_at)
        own, ins = (joined(part_of(*at, 0), part_of(*at, 1)) for at in (own_at, ins_at))
    with jax.named_scope("waitc"):
        got[0].wait_recv()
    with jax.named_scope("fixc1"):
        own_t, outs_t, ins_t = line(own_c, column_of(*outs_at), ins_c, up3, dn3)
        some = applied(own_t, own) + applied(ins_t, ins)
        more = applied(outs_t, part_of(*outs_at, 0))
        for k in range(levels):
            add_ref[pl.ds(k * rows, rows), :] = some[k] + jnp.where(low, more[k], 0.0)
            for dk in range(3):
                tab_ref[pl.ds((dk * levels + k) * rows, rows), :] = outs_t[dk][k]

    with jax.named_scope("fixtop"):

        @pl.when(at_top)
        def _():
            fix_n(True)

    with jax.named_scope("waitc2"):
        got[1].wait_recv()

    with jax.named_scope("end"):
        fold.wait_send()

        @pl.when(inner)
        def _():
            to_s.wait_send()

        all_e.wait_send()
        all_w.wait_send()

        @pl.when(relays)
        def _():
            all_onward.wait_send()


def finish(sizes, part_ref, add_ref, tab_ref, halo_ref, out_ref, stage, sem):
    tracers, levels, rows, lanes, split = sizes
    plane = levels * rows
    slots, pers, shares = layout(tracers, split, levels, lanes)
    lane = lax.broadcasted_iota(jnp.int32, (rows, lanes), 1)
    sides = jnp.logical_or(lane == 0, lane == lanes - 1)
    spot = tracer_of(lane, lanes, tracers)
    add = jnp.stack([add_ref[pl.ds(k * rows, rows), :] for k in range(levels)])

    def rest():
        refs = [halo_ref.at[pl.ds(i * shares[1] * rows, shares[1] * rows)] for i in range(2)]
        values = values_of(refs, (0, 1), jnp.maximum(spot - split, 0), pers[1], slots[1], 0, levels)
        table = [
            jnp.stack([tab_ref[pl.ds((dk * levels + k) * rows, rows), :] for k in range(levels)]) for dk in range(3)
        ]
        return add + applied(table, values)

    with jax.named_scope("insert"):
        terms, full = add, None
        for t in range(tracers):
            if t == EARLY:
                full = rest()
            if t == split:
                terms = full
            for k in range(levels):
                term = pltpu.roll(terms[k], (lanes - 2 * t) % lanes, 1)
                place = pl.ds(t * plane + k * rows, rows)
                stage[place, :] = part_ref[place, :] + jnp.where(sides, term, 0.0)
            if t % STORE == 0 or t == tracers - 1:
                first = 0 if t == 0 else (t - 1) // STORE * STORE + 1
                span = pl.ds(first * plane, (t + 1 - first) * plane)
                pltpu.make_async_copy(stage.at[span], out_ref.at[span], sem).start()
    with jax.named_scope("written"):
        pltpu.make_async_copy(stage, out_ref, sem).wait()


def solution(mesh):
    n_lon, n_lat = mesh.shape["lon"], mesh.shape["lat"]

    def local(tracers, kmt):
        nt, levels, rows, lanes = tracers.shape
        tiles = nt * levels
        split = max(nt - (lanes - 2) // levels, nt // 2)
        cuts = (0, split // 6, split // 2, split, nt)
        groups = tuple(b - a for a, b in zip(cuts, cuts[1:]))
        shares = layout(nt, split, levels, lanes)[-1]
        regs = sum(shares)
        assert levels == rows and groups[0] > 1 and split > EARLY

        def vmem(*shape):
            return pltpu.VMEM(shape, jnp.float32)

        parts = pl.pallas_call(
            functools.partial(kernel, (nt, levels, rows, lanes, n_lon, n_lat, groups)),
            out_shape=[
                vmem(tiles * rows, lanes),
                vmem(levels * rows, lanes),
                vmem(3 * levels * rows, lanes),
                vmem(2 * shares[1] * rows, lanes),
            ],
            in_specs=[pl.BlockSpec(memory_space=pltpu.HBM), pl.BlockSpec(memory_space=pltpu.HBM)],
            out_specs=[pl.BlockSpec(memory_space=pltpu.VMEM)] * 4,
            scratch_shapes=[
                vmem(tiles + levels, rows, lanes),
                pltpu.VMEM((rows, lanes), jnp.int32),
                vmem(15 * levels * rows, lanes),
            ]
            + [vmem(regs * rows, lanes)] * 5
            + [vmem(2 * shares[0] * rows, lanes)]
            + [vmem(tiles + rows, lanes)] * 2
            + [
                pltpu.SemaphoreType.DMA((6,)),
            ],
            compiler_params=pltpu.CompilerParams(collective_id=0, has_side_effects=True),
        )(tracers.reshape(tiles, rows, lanes), kmt)
        parts = [pltpu.with_memory_space_constraint(v, pltpu.VMEM) for v in parts]
        out = pl.pallas_call(
            functools.partial(finish, (nt, levels, rows, lanes, split)),
            out_shape=jax.ShapeDtypeStruct((tiles * rows, lanes), jnp.float32),
            in_specs=[pl.BlockSpec(memory_space=pltpu.VMEM)] * 4,
            out_specs=pl.BlockSpec(memory_space=pltpu.HBM),
            scratch_shapes=[vmem(tiles * rows, lanes), pltpu.SemaphoreType.DMA],
        )(*parts)
        return out.reshape(nt, levels, rows, lanes)

    return jax.shard_map(
        local,
        mesh=mesh,
        in_specs=(P(None, None, "lat", "lon"), P("lat", "lon")),
        out_specs=P(None, None, "lat", "lon"),
        check_vma=False,
    )
```

profile of v0, /device:TPU:0, one launch (start us, length us, event | category | flops | bytes accessed | tf_op | source)
XLA Modules:
  0.0 10.3 jit_solution(10039044032131864411)
XLA Ops:
  0.0 9.2 %shard_map.28 = (f32[2560,128]{1,0:T(8,128)S(1)}, f32[64,128]{1,0:T(8,128)S(1)}, f32[192,128]{1,0:T(8,128)S(1)}, f32[16,128]{1,0:T(8,128)S(1)}) custom-call(f32[320,8,128]{2,1,0:T(8,128)} %bitcast.2, s32[8,128]{1,0:T(8,128)} %kmt_ref.1), custom_call_target="tpu_custom_call" | custom-call | tf_op jit(solution)/shard_map/pallas_call | solution.py:612
  9.2 1.2 %shard_map.29 = f32[2560,128]{1,0:T(8,128)} custom-call(f32[2560,128]{1,0:T(8,128)S(1)} %get-tuple-element.9.part_ref, f32[64,128]{1,0:T(8,128)S(1)} %get-tuple-element.10.add_ref, f32[192,128]{1,0:T(8,128)S(1)} %get-tuple-element.11.tab_ref, f32[16,128]{1,0:T(8,128)S(1)} %get-tuple-element.12.halo_ref), custom_call_target="tpu_custom_call" | custom-call | tf_op jit(solution)/shard_map/pallas_call | solution.py:636
where the time goes:
time: 10.5 us; the launch traced here: 10.3 us
  Pallas kernels  10.3 us (98%)
    pallas_call x1, Pallas kernels, local(): pl.pallas_call(functools.partial(kernel, (nt, levels, rows, lanes, n_lon,...  9.17 us
    pallas_call x1, Pallas kernels, local(): pl.pallas_call(functools.partial(finish, (nt, levels, rows, lanes, split)...  1.16 us

commit v1 on v0

--- a/solution.py
+++ b/solution.py
@@ -17,7 +17,6 @@
 MESH = pl.DeviceIdType.MESH
 TOGETHER = 2
 STORE = 2
-EARLY = 2
 C, E, W, N, S = range(5)
 
 
@@ -81,26 +80,39 @@
     return c[1] * v + c[0] * up3(v) + c[2] * dn3(v)
 
 
-def layout(tracers, split, levels, lanes):
-    slots = (split + 2, tracers - split)
+def layout(splits, levels, lanes):
+    slots = tuple(b - a + (2 if a == 0 else 0) for a, b in zip(splits, splits[1:]))
     pers = tuple((lanes - 2) // slot for slot in slots)
     return slots, pers, tuple((levels + per - 1) // per for per in pers)
 
 
 def tracer_of(lane, lanes, tracers):
-    return jnp.minimum((lane + 1) // 2 % (lanes // 2), tracers - 1)
+    return jnp.minimum(lax.shift_right_logical(lane + 1, 1) & (lanes // 2 - 1), tracers - 1)
 
 
 def both(refs, offs, at, reg):
     rows, lanes = at.shape
     span = pl.ds(reg * rows, rows)
-    west_side = lax.broadcasted_iota(jnp.int32, at.shape, 1) % 2 == 0
-    picked = [pick(ref[span, :], (at + off + lanes) % lanes) for ref, off in zip(refs, offs)]
+    west_side = lax.broadcasted_iota(jnp.int32, at.shape, 1) & 1 == 0
+    wraps = any(off not in (0, 1) for off in offs)
+    index = [at + off & (lanes - 1) if wraps else at + off for off in offs]
+    picked = [pick(ref[span, :], i) for ref, i in zip(refs, index)]
     return jnp.where(west_side, *picked)
 
 
 def values_of(refs, offs, spot, per, slot, first, levels):
     return jnp.stack([both(refs, offs, k % per * slot + spot, first + k // per) for k in range(levels)])
+
+
+def insert_tiles(which, terms, src, dst):
+    levels, rows, lanes = terms.shape
+    lane = lax.broadcasted_iota(jnp.int32, (rows, lanes), 1)
+    sides = jnp.logical_or(lane == 0, lane == lanes - 1)
+    for t in which:
+        for k in range(levels):
+            term = pltpu.roll(terms[k], (lanes - 2 * t) % lanes, 1)
+            place = pl.ds((t * levels + k) * rows, rows)
+            dst[place, :] = src[place, :] + jnp.where(sides, term, 0.0)
 
 
 def kernel(sizes, x_ref, kmt_ref, out_ref, add_ref, tab_ref, halo2, *scratch):
@@ -131,6 +143,8 @@
     early = jnp.logical_and(lon == 0, direct)
     late = jnp.logical_not(early)
     late_top, late_below = jnp.logical_and(late, at_top), jnp.logical_and(late, below_top)
+    urgent = jnp.logical_and(jnp.logical_and(late_below, lon == n_lon - 1), lat % 2 == 0)
+    patient = jnp.logical_and(late_below, jnp.logical_not(urgent))
     e_dev = (lax.rem(lon + 1, n_lon), lat)
     w_dev = (lax.rem(lon + n_lon - 1, n_lon), lat)
     n_dev, s_dev = (lon, lat + 1), (lon, lat - 1)
@@ -140,8 +154,10 @@
     plane = levels * rows
     lead = levels
     ends = [sum(groups[:i]) for i in range(len(groups) + 1)]
-    split = ends[-2]
-    slots, pers, shares = layout(tracers, split, levels, lanes)
+    splits = (0, *ends[2:])
+    split = splits[1]
+    slots, pers, shares = layout(splits, levels, lanes)
+    firsts = [sum(shares[:n]) for n in range(3)]
     kmt_at = pers[0] * slots[0]
 
     load_kmt = pltpu.make_async_copy(kmt_ref, kmt_int, load_sem.at[len(groups)])
@@ -211,16 +227,18 @@
     to_n = rows_of(rows - 1, every, from_s, 0, 1, n_dev)
     to_s = rows_of(0, every, from_n, 1, 0, s_dev)
     to_ss = [rows_of(0, span, from_n, 1, r, s_dev) for span, r in halves]
-    cols = (pl.ds(0, shares[0] * rows), pl.ds(shares[0] * rows, shares[1] * rows))
-    halos = (halo1, halo2)
-    wests = [h.at[pl.ds(0, n * rows)] for h, n in zip(halos, shares)]
-    easts = [h.at[pl.ds(n * rows, n * rows)] for h, n in zip(halos, shares)]
+    cols = [pl.ds(f * rows, n * rows) for f, n in zip(firsts, shares)]
+    tail = sum(shares[1:]) * rows
+    homes = [(halo1, 0, shares[0] * rows), (halo2, 0, tail), (halo2, shares[1] * rows, tail)]
+    wests = [h.at[pl.ds(a, n * rows)] for (h, a, _), n in zip(homes, shares)]
+    easts = [h.at[pl.ds(a + half, n * rows)] for (h, a, half), n in zip(homes, shares)]
+    arrive = (2, 3, 3)
     far_dev = (n_lon - 1, lat_down)
-    to_e = [send(ecol.at[c], wests[i], 2, 2 + i, e_dev) for i, c in enumerate(cols)]
-    to_w = [send(wcol.at[c], easts[i], 3, 2 + i, w_dev) for i, c in enumerate(cols)]
-    onward = [send(relay.at[c], easts[i], 4, 2 + i, far_dev) for i, c in enumerate(cols)]
+    to_e = [send(ecol.at[c], wests[i], 2, arrive[i], e_dev) for i, c in enumerate(cols)]
+    to_w = [send(wcol.at[c], easts[i], 3, arrive[i], w_dev) for i, c in enumerate(cols)]
+    onward = [send(relay.at[c], easts[i], 4, arrive[i], far_dev) for i, c in enumerate(cols)]
     to_relay = send(wcol, relay, 3, 4, (lon, lat_up))
-    got = [send(h, h, 2, 2 + i, e_dev) for i, h in enumerate(halos)]
+    got = [send(h, h, 2, r, e_dev) for h, r in ((halo1, 2), (halo2, 3))]
     all_e, all_w, all_onward = (send(c, relay, s, 4, e_dev) for c, s in ((ecol, 2), (wcol, 3), (relay, 4)))
 
     def tile(t, k):
@@ -230,8 +248,8 @@
         return HALINE * tile(1, k) - THERMAL * tile(0, k)
 
     def where_is(t, k):
-        n, u = (0, t) if t < split else (1, t - split)
-        return k % pers[n] * slots[n] + u, n * shares[0] + k // pers[n]
+        n = sum(t >= s for s in splits[1:])
+        return k % pers[n] * slots[n] + t - splits[n], firsts[n] + k // pers[n]
 
     def gather_columns(e_ref, w_ref, e_off, w_off, before=None, after=None):
         zeros = jnp.zeros((rows, lanes), jnp.float32)
@@ -253,9 +271,9 @@
             for t in range(ends[i], ends[i + 1]):
                 for k in range(levels):
                     place(tile(t, k), *where_is(t, k))
-            if ends[i + 1] in (split, tracers):
-                n = 0 if ends[i + 1] == split else 1
-                for j in range(n * shares[0], n * shares[0] + shares[n]):
+            if ends[i + 1] in splits:
+                n = splits.index(ends[i + 1]) - 1
+                for j in range(firsts[n], firsts[n] + shares[n]):
                     e_ref[pl.ds(j * rows, rows), :] = es[j]
                     w_ref[pl.ds(j * rows, rows), :] = ws[j]
                 if after is not None:
@@ -303,21 +321,26 @@
             def _():
                 folds[i].start()
 
+    def send_part(n, who):
+        @pl.when(who)
+        def _():
+            to_e[n].start()
+
+        @pl.when(jnp.logical_and(who, direct))
+        def _():
+            to_w[n].start()
+
     def after(n):
-        if n == 0:
-
-            @pl.when(late_below)
+        if n < 2:
+
+            @pl.when(patient if n else urgent)
             def _():
                 with jax.named_scope("barrier"):
                     enter()
 
-        @pl.when(late)
-        def _():
-            to_e[n].start()
-
-        @pl.when(jnp.logical_and(late, direct))
-        def _():
-            to_w[n].start()
+        if n == 1:
+            send_part(0, patient)
+        send_part(n, late if n else jnp.logical_and(late, jnp.logical_not(patient)))
 
     with jax.named_scope("loadk"):
         load_kmt.wait()
@@ -501,11 +524,10 @@
             fix_n(False)
 
     spot = tracer_of(lane, lanes, tracers)
-    low = spot < split
-    spots = (jnp.minimum(spot, split - 1), jnp.maximum(spot - split, 0))
 
     def part_of(refs, offs, n):
-        return values_of(refs, offs, spots[n], pers[n], slots[n], n * shares[0], levels)
+        at = jnp.clip(spot - splits[n], 0, splits[n + 1] - splits[n] - 1)
+        return values_of(refs, offs, at, pers[n], slots[n], firsts[n], levels)
 
     def column_of(refs, offs):
         fixed = jnp.zeros((rows, lanes), jnp.int32)
@@ -515,23 +537,27 @@
         wet = jnp.stack([(kmt > float(k)).astype(jnp.float32) for k in range(levels)])
         return column(rho, wet, up3, dn3)
 
-    def joined(first, second):
-        return jnp.stack([jnp.where(low, first[k], second[k]) for k in range(levels)])
+    def joined(*args):
+        a, b, c = (part_of(*args, n) for n in range(3))
+        return jnp.stack([
+            jnp.where(spot < splits[1], a[k], jnp.where(spot < splits[2], b[k], c[k])) for k in range(levels)
+        ])
 
     with jax.named_scope("fixc0"):
         own_at, ins_at, outs_at = ((wcol, ecol), (1, 0)), ((inner_w, inner_e), (2, -1)), ((wests[0], easts[0]), (0, 1))
         own_c, ins_c = column_of(*own_at), column_of(*ins_at)
-        own, ins = (joined(part_of(*at, 0), part_of(*at, 1)) for at in (own_at, ins_at))
+        own, ins = joined(*own_at), joined(*ins_at)
     with jax.named_scope("waitc"):
         got[0].wait_recv()
     with jax.named_scope("fixc1"):
         own_t, outs_t, ins_t = line(own_c, column_of(*outs_at), ins_c, up3, dn3)
         some = applied(own_t, own) + applied(ins_t, ins)
-        more = applied(outs_t, part_of(*outs_at, 0))
+        full = some + applied(outs_t, part_of(*outs_at, 0))
         for k in range(levels):
-            add_ref[pl.ds(k * rows, rows), :] = some[k] + jnp.where(low, more[k], 0.0)
+            add_ref[pl.ds(k * rows, rows), :] = some[k]
             for dk in range(3):
                 tab_ref[pl.ds((dk * levels + k) * rows, rows), :] = outs_t[dk][k]
+        insert_tiles(range(split), full, out_ref, out_ref)
 
     with jax.named_scope("fixtop"):
 
@@ -558,37 +584,41 @@
 
 
 def finish(sizes, part_ref, add_ref, tab_ref, halo_ref, out_ref, stage, sem):
-    tracers, levels, rows, lanes, split = sizes
+    tracers, levels, rows, lanes, splits = sizes
     plane = levels * rows
-    slots, pers, shares = layout(tracers, split, levels, lanes)
+    slots, pers, shares = layout(splits, levels, lanes)
     lane = lax.broadcasted_iota(jnp.int32, (rows, lanes), 1)
-    sides = jnp.logical_or(lane == 0, lane == lanes - 1)
     spot = tracer_of(lane, lanes, tracers)
-    add = jnp.stack([add_ref[pl.ds(k * rows, rows), :] for k in range(levels)])
-
-    def rest():
-        refs = [halo_ref.at[pl.ds(i * shares[1] * rows, shares[1] * rows)] for i in range(2)]
-        values = values_of(refs, (0, 1), jnp.maximum(spot - split, 0), pers[1], slots[1], 0, levels)
+    half = sum(shares[1:]) * rows
+
+    def write(ref, first, count):
+        span = pl.ds(pl.multiple_of(first * plane, plane), count * plane)
+        pltpu.make_async_copy(ref.at[span], out_ref.at[span], sem).start()
+
+    def terms_of(n):
+        refs = [halo_ref.at[pl.ds(i * half, half)] for i in range(2)]
+        at = jnp.clip(spot - splits[n], 0, splits[n + 1] - splits[n] - 1)
+        values = values_of(refs, (0, 1), at, pers[n], slots[n], (n - 1) * shares[1], levels)
         table = [
             jnp.stack([tab_ref[pl.ds((dk * levels + k) * rows, rows), :] for k in range(levels)]) for dk in range(3)
         ]
-        return add + applied(table, values)
+        return jnp.stack([add_ref[pl.ds(k * rows, rows), :] for k in range(levels)]) + applied(table, values)
 
     with jax.named_scope("insert"):
-        terms, full = add, None
-        for t in range(tracers):
-            if t == EARLY:
-                full = rest()
-            if t == split:
-                terms = full
-            for k in range(levels):
-                term = pltpu.roll(terms[k], (lanes - 2 * t) % lanes, 1)
-                place = pl.ds(t * plane + k * rows, rows)
-                stage[place, :] = part_ref[place, :] + jnp.where(sides, term, 0.0)
-            if t % STORE == 0 or t == tracers - 1:
-                first = 0 if t == 0 else (t - 1) // STORE * STORE + 1
-                span = pl.ds(first * plane, (t + 1 - first) * plane)
-                pltpu.make_async_copy(stage.at[span], out_ref.at[span], sem).start()
+        ready = splits[1] // 2
+
+        @pl.loop(0, 2)
+        def _(i):
+            write(part_ref, i * ready, ready)
+
+        terms = [terms_of(1), None]
+        for n in (1, 2):
+            for t in range(splits[n], splits[n + 1], STORE):
+                last = min(t + STORE, splits[n + 1])
+                insert_tiles(range(t, last), terms[n - 1], part_ref, stage)
+                write(stage, t, last - t)
+                if terms[1] is None:
+                    terms[1] = terms_of(2)
     with jax.named_scope("written"):
         pltpu.make_async_copy(stage, out_ref, sem).wait()
 
@@ -599,12 +629,14 @@
     def local(tracers, kmt):
         nt, levels, rows, lanes = tracers.shape
         tiles = nt * levels
-        split = max(nt - (lanes - 2) // levels, nt // 2)
-        cuts = (0, split // 6, split // 2, split, nt)
+        most = (lanes - 2) // levels
+        split = max(nt - most, nt // 2)
+        cuts = (0, split // 6, min(split // 2, max(most - 2, 2)), split, nt)
+        splits = (0, *cuts[2:])
         groups = tuple(b - a for a, b in zip(cuts, cuts[1:]))
-        shares = layout(nt, split, levels, lanes)[-1]
+        shares = layout(splits, levels, lanes)[-1]
         regs = sum(shares)
-        assert levels == rows and groups[0] > 1 and split > EARLY
+        assert levels == rows and groups[0] > 1 and cuts[2] % 2 == 0 and lanes & (lanes - 1) == 0
 
         def vmem(*shape):
             return pltpu.VMEM(shape, jnp.float32)
@@ -615,7 +647,7 @@
                 vmem(tiles * rows, lanes),
                 vmem(levels * rows, lanes),
                 vmem(3 * levels * rows, lanes),
-                vmem(2 * shares[1] * rows, lanes),
+                vmem(2 * sum(shares[1:]) * rows, lanes),
             ],
             in_specs=[pl.BlockSpec(memory_space=pltpu.HBM), pl.BlockSpec(memory_space=pltpu.HBM)],
             out_specs=[pl.BlockSpec(memory_space=pltpu.VMEM)] * 4,
@@ -634,7 +666,7 @@
         )(tracers.reshape(tiles, rows, lanes), kmt)
         parts = [pltpu.with_memory_space_constraint(v, pltpu.VMEM) for v in parts]
         out = pl.pallas_call(
-            functools.partial(finish, (nt, levels, rows, lanes, split)),
+            functools.partial(finish, (nt, levels, rows, lanes, splits)),
             out_shape=jax.ShapeDtypeStruct((tiles * rows, lanes), jnp.float32),
             in_specs=[pl.BlockSpec(memory_space=pltpu.VMEM)] * 4,
             out_specs=pl.BlockSpec(memory_space=pltpu.HBM),

time: 10.5 us -> 10.5 us (level)
  no operation moved by 1% of the time
where the time goes in v1:
time: 10.5 us; the launch traced here: 10.3 us
  Pallas kernels  10.3 us (98%)
    pallas_call x1, Pallas kernels, local(): pl.pallas_call(functools.partial(kernel, (nt, levels, rows, lanes, n_lon,...  9.15 us
    pallas_call x1, Pallas kernels, local(): pl.pallas_call(functools.partial(finish, (nt, levels, rows, lanes, splits...  1.12 us

profile of v1, /device:TPU:0, one launch (start us, length us, event | category | flops | bytes accessed | tf_op | source)
XLA Modules:
  0.0 10.3 jit_solution(392825057157152443)
XLA Ops:
  0.0 9.1 %shard_map.28 = (f32[2560,128]{1,0:T(8,128)S(1)}, f32[64,128]{1,0:T(8,128)S(1)}, f32[192,128]{1,0:T(8,128)S(1)}, f32[32,128]{1,0:T(8,128)S(1)}) custom-call(f32[320,8,128]{2,1,0:T(8,128)} %bitcast.2, s32[8,128]{1,0:T(8,128)} %kmt_ref.1), custom_call_target="tpu_custom_call" | custom-call | tf_op jit(solution)/shard_map/pallas_call | solution.py:644
  9.2 1.1 %shard_map.29 = f32[2560,128]{1,0:T(8,128)} custom-call(f32[2560,128]{1,0:T(8,128)S(1)} %get-tuple-element.9.part_ref, f32[64,128]{1,0:T(8,128)S(1)} %get-tuple-element.10.add_ref, f32[192,128]{1,0:T(8,128)S(1)} %get-tuple-element.11.tab_ref, f32[32,128]{1,0:T(8,128)S(1)} %get-tuple-element.12.halo_ref), custom_call_target="tpu_custom_call" | custom-call | tf_op jit(solution)/shard_map/pallas_call | solution.py:668

commit v2 on v1

--- a/solution.py
+++ b/solution.py
@@ -125,7 +125,7 @@
 
 def body(
     sizes, x_ref, kmt_ref, out_ref, add_ref, tab_ref, halo2,
-    xv, kmt_int, coef, wcol, ecol, inner_w, inner_e, relay, halo1, from_n, from_s,
+    xv, kmt_int, coef, wcol, ecol, inner_w, inner_e, relay, halo0, halo1, from_n, from_s,
     recv_sem, load_sem, send_sem,
 ):
     tracers, levels, rows, lanes, n_lon, n_lat, groups = sizes
@@ -228,17 +228,16 @@
     to_s = rows_of(0, every, from_n, 1, 0, s_dev)
     to_ss = [rows_of(0, span, from_n, 1, r, s_dev) for span, r in halves]
     cols = [pl.ds(f * rows, n * rows) for f, n in zip(firsts, shares)]
-    tail = sum(shares[1:]) * rows
-    homes = [(halo1, 0, shares[0] * rows), (halo2, 0, tail), (halo2, shares[1] * rows, tail)]
-    wests = [h.at[pl.ds(a, n * rows)] for (h, a, _), n in zip(homes, shares)]
-    easts = [h.at[pl.ds(a + half, n * rows)] for (h, a, half), n in zip(homes, shares)]
-    arrive = (2, 3, 3)
+    halos = (halo0, halo1, halo2)
+    wests = [h.at[pl.ds(0, n * rows)] for h, n in zip(halos, shares)]
+    easts = [h.at[pl.ds(n * rows, n * rows)] for h, n in zip(halos, shares)]
+    arrive = (2, 3, 6)
     far_dev = (n_lon - 1, lat_down)
     to_e = [send(ecol.at[c], wests[i], 2, arrive[i], e_dev) for i, c in enumerate(cols)]
     to_w = [send(wcol.at[c], easts[i], 3, arrive[i], w_dev) for i, c in enumerate(cols)]
     onward = [send(relay.at[c], easts[i], 4, arrive[i], far_dev) for i, c in enumerate(cols)]
     to_relay = send(wcol, relay, 3, 4, (lon, lat_up))
-    got = [send(h, h, 2, r, e_dev) for h, r in ((halo1, 2), (halo2, 3))]
+    got = [send(h, h, 2, r, e_dev) for h, r in zip(halos, arrive)]
     all_e, all_w, all_onward = (send(c, relay, s, 4, e_dev) for c, s in ((ecol, 2), (wcol, 3), (relay, 4)))
 
     def tile(t, k):
@@ -525,9 +524,9 @@
 
     spot = tracer_of(lane, lanes, tracers)
 
-    def part_of(refs, offs, n):
+    def part_of(refs, offs, n, first=None):
         at = jnp.clip(spot - splits[n], 0, splits[n + 1] - splits[n] - 1)
-        return values_of(refs, offs, at, pers[n], slots[n], firsts[n], levels)
+        return values_of(refs, offs, at, pers[n], slots[n], firsts[n] if first is None else first, levels)
 
     def column_of(refs, offs):
         fixed = jnp.zeros((rows, lanes), jnp.int32)
@@ -553,20 +552,22 @@
         own_t, outs_t, ins_t = line(own_c, column_of(*outs_at), ins_c, up3, dn3)
         some = applied(own_t, own) + applied(ins_t, ins)
         full = some + applied(outs_t, part_of(*outs_at, 0))
+    with jax.named_scope("waitc1"):
+        got[1].wait_recv()
+    with jax.named_scope("insert0"):
+        more = some + applied(outs_t, part_of((wests[1], easts[1]), (0, 1), 1, 0))
+        insert_tiles(range(split), full, out_ref, out_ref)
         for k in range(levels):
-            add_ref[pl.ds(k * rows, rows), :] = some[k]
+            add_ref[pl.ds(k * rows, rows), :] = more[k]
+            add_ref[pl.ds((levels + k) * rows, rows), :] = some[k]
             for dk in range(3):
                 tab_ref[pl.ds((dk * levels + k) * rows, rows), :] = outs_t[dk][k]
-        insert_tiles(range(split), full, out_ref, out_ref)
 
     with jax.named_scope("fixtop"):
 
         @pl.when(at_top)
         def _():
             fix_n(True)
-
-    with jax.named_scope("waitc2"):
-        got[1].wait_recv()
 
     with jax.named_scope("end"):
         fold.wait_send()
@@ -581,6 +582,9 @@
         @pl.when(relays)
         def _():
             all_onward.wait_send()
+
+    with jax.named_scope("waitc2"):
+        got[2].wait_recv()
 
 
 def finish(sizes, part_ref, add_ref, tab_ref, halo_ref, out_ref, stage, sem):
@@ -589,20 +593,20 @@
     slots, pers, shares = layout(splits, levels, lanes)
     lane = lax.broadcasted_iota(jnp.int32, (rows, lanes), 1)
     spot = tracer_of(lane, lanes, tracers)
-    half = sum(shares[1:]) * rows
+    half = shares[2] * rows
 
     def write(ref, first, count):
         span = pl.ds(pl.multiple_of(first * plane, plane), count * plane)
         pltpu.make_async_copy(ref.at[span], out_ref.at[span], sem).start()
 
-    def terms_of(n):
+    def eight(ref, n):
+        return jnp.stack([ref[pl.ds((n * levels + k) * rows, rows), :] for k in range(levels)])
+
+    def last_terms():
         refs = [halo_ref.at[pl.ds(i * half, half)] for i in range(2)]
-        at = jnp.clip(spot - splits[n], 0, splits[n + 1] - splits[n] - 1)
-        values = values_of(refs, (0, 1), at, pers[n], slots[n], (n - 1) * shares[1], levels)
-        table = [
-            jnp.stack([tab_ref[pl.ds((dk * levels + k) * rows, rows), :] for k in range(levels)]) for dk in range(3)
-        ]
-        return jnp.stack([add_ref[pl.ds(k * rows, rows), :] for k in range(levels)]) + applied(table, values)
+        at = jnp.clip(spot - splits[2], 0, splits[3] - splits[2] - 1)
+        values = values_of(refs, (0, 1), at, pers[2], slots[2], 0, levels)
+        return eight(add_ref, 1) + applied([eight(tab_ref, dk) for dk in range(3)], values)
 
     with jax.named_scope("insert"):
         ready = splits[1] // 2
@@ -611,14 +615,14 @@
         def _(i):
             write(part_ref, i * ready, ready)
 
-        terms = [terms_of(1), None]
+        terms = [eight(add_ref, 0), None]
         for n in (1, 2):
             for t in range(splits[n], splits[n + 1], STORE):
                 last = min(t + STORE, splits[n + 1])
                 insert_tiles(range(t, last), terms[n - 1], part_ref, stage)
                 write(stage, t, last - t)
                 if terms[1] is None:
-                    terms[1] = terms_of(2)
+                    terms[1] = last_terms()
     with jax.named_scope("written"):
         pltpu.make_async_copy(stage, out_ref, sem).wait()
 
@@ -645,9 +649,9 @@
             functools.partial(kernel, (nt, levels, rows, lanes, n_lon, n_lat, groups)),
             out_shape=[
                 vmem(tiles * rows, lanes),
-                vmem(levels * rows, lanes),
+                vmem(2 * levels * rows, lanes),
                 vmem(3 * levels * rows, lanes),
-                vmem(2 * sum(shares[1:]) * rows, lanes),
+                vmem(2 * shares[2] * rows, lanes),
             ],
             in_specs=[pl.BlockSpec(memory_space=pltpu.HBM), pl.BlockSpec(memory_space=pltpu.HBM)],
             out_specs=[pl.BlockSpec(memory_space=pltpu.VMEM)] * 4,
@@ -657,10 +661,10 @@
                 vmem(15 * levels * rows, lanes),
             ]
             + [vmem(regs * rows, lanes)] * 5
-            + [vmem(2 * shares[0] * rows, lanes)]
+            + [vmem(2 * n * rows, lanes) for n in shares[:2]]
             + [vmem(tiles + rows, lanes)] * 2
             + [
-                pltpu.SemaphoreType.DMA((6,)),
+                pltpu.SemaphoreType.DMA((7,)),
             ],
             compiler_params=pltpu.CompilerParams(collective_id=0, has_side_effects=True),
         )(tracers.reshape(tiles, rows, lanes), kmt)

time: 10.5 us -> 10.4 us (level)
  no operation moved by 1% of the time
where the time goes in v2:
time: 10.4 us; the launch traced here: 10.2 us
  Pallas kernels  10.2 us (98%)
    pallas_call x1, Pallas kernels, local(): pl.pallas_call(functools.partial(kernel, (nt, levels, rows, lanes, n_lon,...  9.17 us
    pallas_call x1, Pallas kernels, local(): pl.pallas_call(functools.partial(finish, (nt, levels, rows, lanes, splits...  1.05 us

profile of v2, /device:TPU:0, one launch (start us, length us, event | category | flops | bytes accessed | tf_op | source)
XLA Modules:
  0.0 10.2 jit_solution(12539541063210938503)
XLA Ops:
  0.0 9.2 %shard_map.28 = (f32[2560,128]{1,0:T(8,128)S(1)}, f32[128,128]{1,0:T(8,128)S(1)}, f32[192,128]{1,0:T(8,128)S(1)}, f32[16,128]{1,0:T(8,128)S(1)}) custom-call(f32[320,8,128]{2,1,0:T(8,128)} %bitcast.2, s32[8,128]{1,0:T(8,128)} %kmt_ref.1), custom_call_target="tpu_custom_call" | custom-call | tf_op jit(solution)/shard_map/pallas_call | solution.py:648
  9.2 1.0 %shard_map.29 = f32[2560,128]{1,0:T(8,128)} custom-call(f32[2560,128]{1,0:T(8,128)S(1)} %get-tuple-element.9.part_ref, f32[128,128]{1,0:T(8,128)S(1)} %get-tuple-element.10.add_ref, f32[192,128]{1,0:T(8,128)S(1)} %get-tuple-element.11.tab_ref, f32[16,128]{1,0:T(8,128)S(1)} %get-tuple-element.12.halo_ref), custom_call_target="tpu_custom_call" | custom-call | tf_op jit(solution)/shard_map/pallas_call | solution.py:672

commit v3 on v2

--- a/solution.py
+++ b/solution.py
@@ -214,24 +214,21 @@
     def rows_of(r, span, dst, s, into, dev):
         return send(xv.at[span, r, :], dst.at[span], s, into, dev)
 
-    cut = lead + ends[-2] * levels
     starts = [lead - 1] + [lead + e * levels for e in ends[1:]]
     spans = [pl.ds(a, b - a) for a, b in zip(starts, starts[1:])]
     every = pl.ds(lead - 1, tiles + 1)
-    halves = [(pl.ds(lead - 1, cut - lead + 1), 0), (spans[-1], 5)]
     fold = rows_of(rows - 1, every, from_n, 0, 0, fold_dev)
     folds = [
-        rows_of(rows - 1, span, from_n, 0, 5 if i == len(spans) - 1 else 0, fold_dev)
-        for i, span in enumerate(spans)
+        rows_of(rows - 1, span, from_n, 0, 0, fold_dev)
+        for span in spans
     ]
     to_n = rows_of(rows - 1, every, from_s, 0, 1, n_dev)
     to_s = rows_of(0, every, from_n, 1, 0, s_dev)
-    to_ss = [rows_of(0, span, from_n, 1, r, s_dev) for span, r in halves]
     cols = [pl.ds(f * rows, n * rows) for f, n in zip(firsts, shares)]
     halos = (halo0, halo1, halo2)
     wests = [h.at[pl.ds(0, n * rows)] for h, n in zip(halos, shares)]
     easts = [h.at[pl.ds(n * rows, n * rows)] for h, n in zip(halos, shares)]
-    arrive = (2, 3, 6)
+    arrive = (2, 3, 5)
     far_dev = (n_lon - 1, lat_down)
     to_e = [send(ecol.at[c], wests[i], 2, arrive[i], e_dev) for i, c in enumerate(cols)]
     to_w = [send(wcol.at[c], easts[i], 3, arrive[i], w_dev) for i, c in enumerate(cols)]
@@ -302,8 +299,7 @@
 
         @pl.when(inner)
         def _():
-            for copy in to_ss:
-                copy.start()
+            to_s.start()
 
     def before(i):
         with jax.named_scope(f"load{i}"):
@@ -489,7 +485,7 @@
             if n:
                 wait()
             count = last - first
-            batch = count if turn else next(b for b in (8, 5, 4, 3, 2, 1) if count % b == 0)
+            batch = next(b for b in (20, 10, 8, 5, 4, 3, 2, 1) if count % b == 0 and (turn or b <= 8))
 
             @pl.loop(0, count // batch)
             def _(i, first=first, batch=batch):
@@ -505,8 +501,7 @@
                     )
 
     def fix_n(turn):
-        parts = [(0, ends[-2], to_ss[0].wait_recv), (ends[-2], tracers, to_ss[1].wait_recv)]
-        fix_rows(from_n, rows - 1, rows - 2, True, turn, parts)
+        fix_rows(from_n, rows - 1, rows - 2, True, turn, [(0, tracers, to_s.wait_recv)])
 
     with jax.named_scope("fixs"):
 
@@ -664,7 +659,7 @@
             + [vmem(2 * n * rows, lanes) for n in shares[:2]]
             + [vmem(tiles + rows, lanes)] * 2
             + [
-                pltpu.SemaphoreType.DMA((7,)),
+                pltpu.SemaphoreType.DMA((6,)),
             ],
             compiler_params=pltpu.CompilerParams(collective_id=0, has_side_effects=True),
         )(tracers.reshape(tiles, rows, lanes), kmt)

time: 10.4 us -> 10.4 us (level)
  no operation moved by 1% of the time
where the time goes in v3:
time: 10.4 us; the launch traced here: 10.2 us
  Pallas kernels  10.2 us (98%)
    pallas_call x1, Pallas kernels, local(): pl.pallas_call(functools.partial(kernel, (nt, levels, rows, lanes, n_lon,...  9.16 us
    pallas_call x1, Pallas kernels, local(): pl.pallas_call(functools.partial(finish, (nt, levels, rows, lanes, splits...  1.05 us

profile of v3, /device:TPU:0, one launch (start us, length us, event | category | flops | bytes accessed | tf_op | source)
XLA Modules:
  0.0 10.2 jit_solution(15942666745602965235)
XLA Ops:
  0.0 9.2 %shard_map.28 = (f32[2560,128]{1,0:T(8,128)S(1)}, f32[128,128]{1,0:T(8,128)S(1)}, f32[192,128]{1,0:T(8,128)S(1)}, f32[16,128]{1,0:T(8,128)S(1)}) custom-call(f32[320,8,128]{2,1,0:T(8,128)} %bitcast.2, s32[8,128]{1,0:T(8,128)} %kmt_ref.1), custom_call_target="tpu_custom_call" | custom-call | tf_op jit(solution)/shard_map/pallas_call | solution.py:643
  9.2 1.0 %shard_map.29 = f32[2560,128]{1,0:T(8,128)} custom-call(f32[2560,128]{1,0:T(8,128)S(1)} %get-tuple-element.9.part_ref, f32[128,128]{1,0:T(8,128)S(1)} %get-tuple-element.10.add_ref, f32[192,128]{1,0:T(8,128)S(1)} %get-tuple-element.11.tab_ref, f32[16,128]{1,0:T(8,128)S(1)} %get-tuple-element.12.halo_ref), custom_call_target="tpu_custom_call" | custom-call | tf_op jit(solution)/shard_map/pallas_call | solution.py:667

commit v4 on v2

--- a/solution.py
+++ b/solution.py
@@ -16,7 +16,7 @@
 
 MESH = pl.DeviceIdType.MESH
 TOGETHER = 2
-STORE = 2
+STORE = 4
 C, E, W, N, S = range(5)
 
 

time: 10.4 us -> 10.5 us (level)
  no operation moved by 1% of the time
where the time goes in v4:
time: 10.5 us; the launch traced here: 10.2 us
  Pallas kernels  10.2 us (97%)
    pallas_call x1, Pallas kernels, local(): pl.pallas_call(functools.partial(kernel, (nt, levels, rows, lanes, n_lon,...  9.17 us
    pallas_call x1, Pallas kernels, local(): pl.pallas_call(functools.partial(finish, (nt, levels, rows, lanes, splits...  1.07 us

profile of v4, /device:TPU:0, one launch (start us, length us, event | category | flops | bytes accessed | tf_op | source)
XLA Modules:
  0.0 10.2 jit_solution(11124514694911933761)
XLA Ops:
  0.0 9.2 %shard_map.28 = (f32[2560,128]{1,0:T(8,128)S(1)}, f32[128,128]{1,0:T(8,128)S(1)}, f32[192,128]{1,0:T(8,128)S(1)}, f32[16,128]{1,0:T(8,128)S(1)}) custom-call(f32[320,8,128]{2,1,0:T(8,128)} %bitcast.2, s32[8,128]{1,0:T(8,128)} %kmt_ref.1), custom_call_target="tpu_custom_call" | custom-call | tf_op jit(solution)/shard_map/pallas_call | solution.py:648
  9.2 1.1 %shard_map.29 = f32[2560,128]{1,0:T(8,128)} custom-call(f32[2560,128]{1,0:T(8,128)S(1)} %get-tuple-element.9.part_ref, f32[128,128]{1,0:T(8,128)S(1)} %get-tuple-element.10.add_ref, f32[192,128]{1,0:T(8,128)S(1)} %get-tuple-element.11.tab_ref, f32[16,128]{1,0:T(8,128)S(1)} %get-tuple-element.12.halo_ref), custom_call_target="tpu_custom_call" | custom-call | tf_op jit(solution)/shard_map/pallas_call | solution.py:672
